TPU v7x, 32 devices: a whole 2x2x4 slice. The times are simulated.
32 devices in a mesh: face: 8 (over z, core), sub: 4 (over y, x).
Axes of the slice: x: 2, y: 2, z: 4, core: 2. Of those that a mesh axis runs over, the one named last changes fastest.
Arguments:
- mesh_latent: bfloat16 [8192, 512], P(('face', 'sub')), may hold values from -6 to 6
- edge_latent: bfloat16 [65536, 512], P(('face', 'sub')), may hold values from -6 to 6
- grid_features: bfloat16 [8192, 384], P(('face', 'sub')), may hold values from -6 to 6
- senders: int32 [65536], P(('face', 'sub')), may hold values from 0 to 383, as said below
- receivers: int32 [65536], P(('face', 'sub')), may hold values from 0 to 255
- send_lists: int32 [32, 4, 32], P(('face', 'sub')), may hold values from -1 to 255, as said below
- link_sources: int32 [16384], P(('face', 'sub')), may hold values from 0 to 255
- link_targets: int32 [16384], P(('face', 'sub')), may hold values from 0 to 255
- node_area: float32 [8192], P(('face', 'sub')), may hold values from 0.25 to 4.5
- grid_weight: bfloat16 [384, 512], P(None, 'sub'), may hold values from -0.3125 to 0.3125
- encode_weight: bfloat16 [1024, 512], P('sub'), may hold values from -0.1875 to 0.1875
- edge_first: bfloat16 [1, 1536, 512], P(None, 'sub'), may hold values from -0.15625 to 0.15625
- edge_second: bfloat16 [1, 512, 512], P(None, 'sub'), may hold values from -0.25 to 0.25
- node_first: bfloat16 [1, 1024, 512], P(None, 'sub'), may hold values from -0.1875 to 0.1875
- node_second: bfloat16 [1, 512, 512], P(None, 'sub'), may hold values from -0.25 to 0.25
Outputs:
- mesh_result: bfloat16 [8192, 512], P(('face', 'sub'))
- edge_result: bfloat16 [65536, 512], P(('face', 'sub'))
- masses: float32 [1, 512], replicated
Inputs may be any that keep to these rules, and one draw needn't show every extreme that they name: `send_lists`: entries are the sending partition's own node numbers, or -1 for an unused slot; in every list the used slots come first, hold distinct nodes and number 32 // 2 or more; for every list number some partition uses all 32 slots. `senders`: A value below 256 names one of the partition's own nodes; 256 + d * 32 + k names slot k of the list with number d that the partition receives, and that slot is always a used one.
All inputs are finite; a program needn't handle non-finite values.
Results may differ from a plain program's by a relative error of at most 0.008.
Values may be sent and summed in bfloat16 or wider, within the bound.
A program may use at most 64 MiB of HBM per device.

v0:
```python
import jax
import jax.numpy as jnp
from jax import lax
from jax.sharding import PartitionSpec as P


def passed_along(value, axis, steps):
    count = lax.axis_size(axis)
    pairs = [(source, (source + steps) % count) for source in range(count)]
    return lax.ppermute(value, axis, pairs)


def fold_rows(weight, operand):
    return jnp.dot(
        operand,
        lax.all_gather(weight, "sub", axis=0, tiled=True),
        preferred_element_type=jnp.float32,
    )


def edge_rows(weight, operand):
    storage = jnp.zeros((1, weight.shape[1]), jnp.bfloat16)
    total = jnp.dot(
        operand,
        lax.all_gather(weight, "sub", axis=0, tiled=True),
        preferred_element_type=jnp.float32,
    )
    return (total, storage)


def along_face(values, offset):
    return passed_along(values, "face", offset)


def along_sub(values, offset):
    return passed_along(values, "sub", offset)


def per_device(
    mesh_latent,
    edge_latent,
    grid_features,
    senders,
    receivers,
    send_lists,
    link_sources,
    link_targets,
    node_area,
    grid_weight,
    encode_weight,
    edge_first,
    edge_second,
    node_first,
    node_second,
):
    node_rows = mesh_latent.shape[0]
    nodes_all = node_rows * lax.axis_size("face") * lax.axis_size("sub")
    grid_latent = jax.nn.silu(
        jnp.dot(
            grid_features,
            lax.all_gather(grid_weight, "sub", axis=1, tiled=True),
            preferred_element_type=jnp.float32,
        )
    ).astype(jnp.bfloat16)

    def project(weight, operand):
        return fold_rows(weight, operand)

    node_ids = jnp.arange(node_rows, dtype=jnp.int32)
    joined = jnp.concatenate(
        [jnp.take(grid_latent, link_sources, axis=0), jnp.take(mesh_latent, link_targets, axis=0)],
        axis=1,
    )
    messages = jax.nn.silu(project(encode_weight, joined)).astype(jnp.bfloat16)
    target_onehot = (link_targets[:, None] == node_ids[None, :]).astype(jnp.bfloat16)
    arriving = lax.dot_general(
        target_onehot, messages, (((0,), (0,)), ((), ())), preferred_element_type=jnp.float32
    )
    latent = (mesh_latent.astype(jnp.float32) + arriving).astype(jnp.bfloat16)
    halo_lists = send_lists[0]
    list_mask = (halo_lists >= 0)[:, :, None]
    receive_onehot = (receivers[:, None] == node_ids[None, :]).astype(jnp.bfloat16)
    edge_state = edge_latent
    picked = jnp.take(latent, jnp.maximum(halo_lists, 0), axis=0)
    picked = jnp.where(list_mask, picked, jnp.zeros((), jnp.bfloat16))
    lower_face = along_face(picked[0], 1)
    upper_face = along_face(picked[1], -1)
    lower_sub = along_sub(picked[2], 1)
    upper_sub = along_sub(picked[3], -1)
    arrived = jnp.concatenate([lower_face, upper_face, lower_sub, upper_sub], axis=0)
    receiving_rows = jnp.take(latent, receivers, axis=0)
    node_table = jnp.concatenate([latent, arrived], axis=0)
    inputs = jnp.concatenate(
        [edge_state, jnp.take(node_table, senders, axis=0), receiving_rows], axis=1
    )
    before, unused_rows = edge_rows(edge_first[0], inputs)
    hidden = jax.nn.silu(before).astype(jnp.bfloat16)
    edge_state = (edge_state.astype(jnp.float32) + project(edge_second[0], hidden)).astype(
        jnp.bfloat16
    )
    incoming = lax.dot_general(
        receive_onehot, edge_state, (((0,), (0,)), ((), ())), preferred_element_type=jnp.float32
    ).astype(jnp.bfloat16)
    node_hidden = jax.nn.silu(
        project(node_first[0], jnp.concatenate([latent, incoming], axis=1))
    ).astype(jnp.bfloat16)
    latent = (latent.astype(jnp.float32) + project(node_second[0], node_hidden)).astype(
        jnp.bfloat16
    )
    totals = [jnp.dot(node_area, latent.astype(jnp.float32), precision=lax.Precision.HIGHEST)]
    stacked = lax.psum(jnp.stack(totals), ("face", "sub"))
    masses = stacked / nodes_all
    return (latent, edge_state, masses)


def solution(mesh):
    in_specs = (
        P(("face", "sub"), None),
        P(("face", "sub"), None),
        P(("face", "sub"), None),
        P(("face", "sub")),
        P(("face", "sub")),
        P(("face", "sub"), None, None),
        P(("face", "sub")),
        P(("face", "sub")),
        P(("face", "sub")),
        P(None, "sub"),
        P("sub", None),
        P(None, "sub", None),
        P(None, "sub", None),
        P(None, "sub", None),
        P(None, "sub", None),
    )
    out_specs = (P(("face", "sub"), None), P(("face", "sub"), None), P())
    return jax.shard_map(
        per_device, mesh=mesh, in_specs=in_specs, out_specs=out_specs, check_vma=False
    )
```

profile of v0, /device:TPU:0, one launch (start us, length us, event | category | flops | bytes accessed | tf_op | source)
XLA Modules:
  0.0 153.9 jit_solution(15797503033091889898)
XLA Ops:
  7.2 0.7 all-gather.8.cloned.1.call-update
  8.0 0.7 all-gather.10.cloned.1.call-update
  9.4 0.7 compare_select_fusion.2
  10.1 0.7 compare_and_fusion.2
  10.8 0.7 compare_select_fusion.3
  11.5 0.7 compare_and_fusion.3
  12.2 0.7 broadcast_maximum_fusion
  12.8 0.7 compare_bitcast_fusion.1
  13.5 0.7 fusion.46
  14.2 1.3 compare_and_fusion.1
  15.5 0.7 fusion.47
  16.2 1.3 compare_and_fusion
  17.5 12.5 %all_gather.18 = bf16[384,512]{1,0:T(8,128)(2,1)S(1)} all-gather(bf16[384,128]{1,0:T(8,128)(2,1)} %param.26), channel_id=1, replica_groups=mesh['face'=8,'sub'=4] {'sub'}, dimensions={1}, use_global_device_ids=true | all-gather | bytes 491520 | tf_op jit(solution)/shard_map/all_gather | solution.py:61
  30.1 13.3 %all-gather.1 = bf16[1,512,512]{2,1,0:T(8,128)(2,1)} all-gather(bf16[1,128,512]{2,1,0:T(8,128)(2,1)} %param.29), channel_id=3, replica_groups=mesh['face'=8,'sub'=4] {'sub'}, dimensions={1}, use_global_device_ids=true | all-gather | bytes 655360 | tf_op jit(solution)/shard_map/all_gather | solution.py:16
  43.5 10.7 %all-gather.3 = bf16[1,512,512]{2,1,0:T(8,128)(2,1)S(1)} all-gather(bf16[1,128,512]{2,1,0:T(8,128)(2,1)S(1)} %copy-done.3), channel_id=5, replica_groups=mesh['face'=8,'sub'=4] {'sub'}, dimensions={1}, use_global_device_ids=true | all-gather | bytes 655360 | tf_op jit(solution)/shard_map/all_gather | solution.py:16
  54.6 2.0 %gather_fusion.3 = bf16[512,512]{1,0:T(8,128)(2,1)S(1)} fusion(bf16[256,512]{1,0:T(8,128)(2,1)S(1)} %multiply_convert_fusion.4, s32[1024]{0:T(1024)S(1)} %pad_clamp_fusion.2), kind=kCustom, calls=%fused_computation.clone | custom fusion | bytes 1050624 | tf_op jit(solution)/shard_map/jit(_take)/gather | solution.py:71
  56.6 2.0 %gather_fusion.4 = bf16[512,512]{1,0:T(8,128)(2,1)S(1)} fusion(bf16[256,512]{1,0:T(8,128)(2,1)S(1)} %copy-done.1, s32[1024]{0:T(1024)S(1)} %pad_clamp_fusion.1), kind=kCustom, calls=%fused_computation.1.clone | custom fusion | bytes 1050624 | tf_op jit(solution)/shard_map/jit(_take)/gather | solution.py:71
  59.2 2.3 %constant_dynamic-update-slice_fusion.4 = (bf16[384,512]{1,0:T(8,128)(2,1)S(1)}, bf16[256,512]{1,0:T(8,128)(2,1)S(1)}) fusion(bf16[1024,512]{1,0:T(8,128)(2,1)} %all-gather.8.cloned.1.call-done, bf16[512,512]{1,0:T(8,128)(2,1)S(1)} %get-tuple-element.12, bf16[512,512]{1,0:T(8,128)(2,1)S(1)} %get-tuple-element.13, s32[512]{0:T(512)S(1)} %copy-done.6, ...), kind=kOutput, calls=%fused_computation.55 | convolution fusion | flops 675020800 | bytes 2885632 | tf_op jit(solution)/shard_map/dot_general | solution.py:76
  61.5 0.8 gather_fusion
  63.1 3.5 %collective-permute-start.1 = (bf16[32,512]{1,0:T(8,128)(2,1)}, bf16[32,512]{1,0:T(8,128)(2,1)}, u32[]{:S(2)}, u32[]{:S(2)}) collective-permute-start(bf16[32,512]{1,0:T(8,128)(2,1)} %get-tuple-element.6), channel_id=1, source_target_pairs={{0,28},{4,0},{8,4},{12,8},{16,12},{20,16},{24,20},{28,24},{1,29},{... | collective-permute-start | bytes 98312 | tf_op jit(solution)/shard_map/ppermute | solution.py:10
  67.1 2.5 %collective-permute-start.3 = (bf16[32,512]{1,0:T(8,128)(2,1)}, bf16[32,512]{1,0:T(8,128)(2,1)S(1)}, u32[]{:S(2)}, u32[]{:S(2)}) collective-permute-start(bf16[32,512]{1,0:T(8,128)(2,1)} %get-tuple-element.4), channel_id=1, source_target_pairs={{0,3},{1,0},{2,1},{3,2},{4,7},{5,4},{6,5},{7,6},{8,11},{9,8},{10,9... | collective-permute-start | bytes 98312 | tf_op jit(solution)/shard_map/ppermute | solution.py:10
  69.6 7.5 %gather_fusion.2 = bf16[2048,512]{1,0:T(8,128)(2,1)S(1)} fusion(bf16[256,512]{1,0:T(8,128)(2,1)S(1)} %get-tuple-element.11, s32[2048]{0:T(1024)S(1)} %fusion.47), kind=kCustom, calls=%fused_computation.4 | custom fusion | bytes 4202496 | tf_op jit(solution)/shard_map/jit(_take)/gather | solution.py:91
  77.1 2.2 %broadcast_select_fusion = bf16[2048,512]{1,0:T(8,128)(2,1)} fusion(bf16[2048,512]{1,0:T(8,128)(2,1)S(1)} %gather_fusion.2, pred[2048]{0:T(1024)(128)(4,1)} %compare_and_fusion), kind=kLoop, calls=%fused_computation.14 | loop fusion | flops 1048576 | bytes 4196352 | tf_op jit(solution)/shard_map/jit(_take)/select_n | solution.py:91
  79.4 0.8 constant_dynamic-update-slice_fusion.3
  80.1 0.8 constant_dynamic-update-slice_fusion.2
  80.9 7.5 %gather_fusion.1 = bf16[2048,512]{1,0:T(8,128)(2,1)S(1)} fusion(bf16[384,512]{1,0:T(8,128)(2,1)S(1)} %constant_dynamic-update-slice_fusion, s32[2048]{0:T(1024)S(1)} %fusion.46), kind=kCustom, calls=%fused_computation.3 | custom fusion | bytes 4202496 | tf_op jit(solution)/shard_map/jit(_take)/gather | solution.py:94
  88.5 1.6 %broadcast_select_fusion.1 = bf16[2048,512]{1,0:T(8,128)(2,1)} fusion(bf16[2048,512]{1,0:T(8,128)(2,1)S(1)} %gather_fusion.1, pred[2048]{0:T(1024)(128)(4,1)S(1)} %copy-done.5), kind=kLoop, calls=%fused_computation.15 | loop fusion | flops 1048576 | bytes 4196352 | tf_op jit(solution)/shard_map/jit(_take)/select_n | solution.py:94
  90.0 8.5 %add_convert_fusion = bf16[2048,512]{1,0:T(8,128)(2,1)S(1)} fusion(bf16[2048,512]{1,0:T(8,128)(2,1)} %param.18, bf16[2048,512]{1,0:T(8,128)(2,1)} %broadcast_select_fusion, bf16[2048,512]{1,0:T(8,128)(2,1)} %broadcast_select_fusion.1, bf16[1,1536,512]{2,1,0:T(8,128)(2,1)} %all-gather.10.cloned.1.call-done, bf16[1,512,512]{2,1,0:T(8,128)(2,1)} %all-gather.1), kind=kOutput, calls=%fused_computation.11 | convolution fusion | flops 4322230272 | bytes 10485760 | tf_op jit(solution)/shard_map/dot_general | solution.py:14
  98.6 1.8 %fusion.8 = bf16[256,512]{1,0:T(8,128)(2,1)} fusion(bf16[2048,512]{1,0:T(8,128)(2,1)S(1)} %add_convert_fusion, s32[2048]{0:T(1024)S(1)} %copy-done.4), kind=kOutput, calls=%fused_computation.20 | convolution fusion | flops 537526272 | bytes 2367488 | tf_op jit(solution)/shard_map/dot_general | solution.py:101
  100.4 4.8 %all-gather.12.cloned.1.call-done = bf16[1,1024,512]{2,1,0:T(8,128)(2,1)} async-done(((bf16[1,256,512]{2,1,0:T(8,128)(2,1)}), bf16[1,1024,512]{2,1,0:T(8,128)(2,1)}) %all-gather.12.cloned.1.call-update) | async-done | bytes 1048592 | tf_op jit(solution)/shard_map/all_gather | solution.py:16
  105.3 2.0 %fusion.10 = bf16[256,512]{1,0:T(8,128)(2,1)S(1)} fusion(bf16[1,512,512]{2,1,0:T(8,128)(2,1)S(1)} %all-gather.3, bf16[1,1024,512]{2,1,0:T(8,128)(2,1)} %all-gather.12.cloned.1.call-done, bf16[256,512]{1,0:T(8,128)(2,1)} %fusion.8, bf16[256,512]{1,0:T(8,128)(2,1)S(1)} %get-tuple-element.11), kind=kOutput, calls=%fused_computation.22 | convolution fusion | flops 404750336 | bytes 2359296 | tf_op jit(solution)/shard_map/dot_general | solution.py:14
  107.5 39.2 %psum.7 = f32[1,512]{1,0:T(1,128)S(1)} all-reduce(f32[1,512]{1,0:T(1,128)S(1)} %fusion.59), channel_id=1, replica_groups=mesh['face'=8,'sub'=4] {'face','sub'}, use_global_device_ids=true, to_apply=%region_0.2 | all-reduce | flops 512 | bytes 4096 | tf_op jit(solution)/shard_map/psum | solution.py:111
  (42 shorter events, 3.9 us)
Async XLA Ops:
  7.2 47.0 %copy-start = (bf16[256,384]{1,0:T(8,128)(2,1)S(1)}, bf16[256,384]{1,0:T(8,128)(2,1)}, u32[]{:S(2)}) copy-start(bf16[256,384]{1,0:T(8,128)(2,1)} %param.19) | copy-start | bytes 589828
  7.2 36.3 %copy-start.3 = (bf16[1,128,512]{2,1,0:T(8,128)(2,1)S(1)}, bf16[1,128,512]{2,1,0:T(8,128)(2,1)}, u32[]{:S(2)}) copy-start(bf16[1,128,512]{2,1,0:T(8,128)(2,1)} %param.31) | copy-start | bytes 393220
  7.2 51.6 %all-gather.8.cloned.1.call-start = ((), (), s32[]{:S(2)}) async-start(), calls=%async_computation | async-start | bytes 1310720 | tf_op jit(solution)/shard_map/all_gather | solution.py:16
  7.9 82.1 %all-gather.10.cloned.1.call-start = ((), (), s32[]{:S(2)}) async-start(), calls=%async_computation.1 | async-start | bytes 1966080 | tf_op jit(solution)/shard_map/all_gather | solution.py:25
  8.7 96.6 %all-gather.12.cloned.1.call-start = ((), (), s32[]{:S(2)}) async-start(), calls=%async_computation.2 | async-start | bytes 1310720 | tf_op jit(solution)/shard_map/all_gather | solution.py:16
  54.6 2.0 %copy-start.1 = (bf16[256,512]{1,0:T(8,128)(2,1)S(1)}, bf16[256,512]{1,0:T(8,128)(2,1)}, u32[]{:S(2)}) copy-start(bf16[256,512]{1,0:T(8,128)(2,1)} %param.17) | copy-start | bytes 786436
  58.5 0.7 copy-start.6
  63.1 16.2 %collective-permute-start = (bf16[32,512]{1,0:T(8,128)(2,1)}, bf16[32,512]{1,0:T(8,128)(2,1)}, u32[]{:S(2)}, u32[]{:S(2)}) collective-permute-start(bf16[32,512]{1,0:T(8,128)(2,1)} %get-tuple-element.7), channel_id=1, source_target_pairs={{0,4},{4,8},{8,12},{12,16},{16,20},{20,24},{24,28},{28,0},{1,5},{5... | collective-permute-start | bytes 98312 | tf_op jit(solution)/shard_map/ppermute | solution.py:10
  63.1 17.0 %collective-permute-start.1 = (bf16[32,512]{1,0:T(8,128)(2,1)}, bf16[32,512]{1,0:T(8,128)(2,1)}, u32[]{:S(2)}, u32[]{:S(2)}) collective-permute-start(bf16[32,512]{1,0:T(8,128)(2,1)} %get-tuple-element.6), channel_id=1, source_target_pairs={{0,28},{4,0},{8,4},{12,8},{16,12},{20,16},{24,20},{28,24},{1,29},{... | collective-permute-start | bytes 98312 | tf_op jit(solution)/shard_map/ppermute | solution.py:10
  66.7 14.2 %collective-permute-start.2 = (bf16[32,512]{1,0:T(8,128)(2,1)}, bf16[32,512]{1,0:T(8,128)(2,1)S(1)}, u32[]{:S(2)}, u32[]{:S(2)}) collective-permute-start(bf16[32,512]{1,0:T(8,128)(2,1)} %get-tuple-element.5), channel_id=1, source_target_pairs={{0,1},{1,2},{2,3},{3,0},{4,5},{5,6},{6,7},{7,4},{8,9},{9,10},{10,1... | collective-permute-start | bytes 98312 | tf_op jit(solution)/shard_map/ppermute | solution.py:10
  67.1 13.8 %collective-permute-start.3 = (bf16[32,512]{1,0:T(8,128)(2,1)}, bf16[32,512]{1,0:T(8,128)(2,1)S(1)}, u32[]{:S(2)}, u32[]{:S(2)}) collective-permute-start(bf16[32,512]{1,0:T(8,128)(2,1)} %get-tuple-element.4), channel_id=1, source_target_pairs={{0,3},{1,0},{2,1},{3,2},{4,7},{5,4},{6,5},{7,6},{8,11},{9,8},{10,9... | collective-permute-start | bytes 98312 | tf_op jit(solution)/shard_map/ppermute | solution.py:10
  80.9 7.6 %copy-start.5 = (pred[2048]{0:T(1024)(128)(4,1)S(1)}, pred[2048]{0:T(1024)(128)(4,1)}, u32[]{:S(2)}) copy-start(pred[2048]{0:T(1024)(128)(4,1)} %compare_and_fusion.1) | copy-start | bytes 6148
  90.0 8.5 %copy-start.4 = (s32[2048]{0:T(1024)S(1)}, s32[2048]{0:T(1024)}, u32[]{:S(2)}) copy-start(s32[2048]{0:T(1024)} %param.21) | copy-start | bytes 24580
  98.6 8.7 %copy-start.8 = (bf16[2048,512]{1,0:T(8,128)(2,1)}, bf16[2048,512]{1,0:T(8,128)(2,1)S(1)}, u32[]{:S(2)}) copy-start(bf16[2048,512]{1,0:T(8,128)(2,1)S(1)} %add_convert_fusion) | copy-start | bytes 6291460
  100.4 6.9 %copy-start.7 = (f32[256]{0:T(256)S(1)}, f32[256]{0:T(256)}, u32[]{:S(2)}) copy-start(f32[256]{0:T(256)} %param.25) | copy-start | bytes 3076
  107.3 40.1 %copy-start.2 = (bf16[256,512]{1,0:T(8,128)(2,1)}, bf16[256,512]{1,0:T(8,128)(2,1)S(1)}, u32[]{:S(2)}) copy-start(bf16[256,512]{1,0:T(8,128)(2,1)S(1)} %fusion.10) | copy-start | bytes 786436
Sparse Core Ops, SparseCore 0:
  9.8 32.7 all-gather.7
  44.4 32.7 all-gather.9
  79.1 26.1 all-gather.11
where the time goes:
time: 155 us; the launch traced here: 154 us
  blocking collectives  75.8 us (49%)
  local copies, waits for them, and re-layouts  22.6 us (15%)
  matrix products  15.3 us (10%)
  between operations  14 us (9%)
  other arithmetic  12.7 us (8%)
  waiting for transfers between devices  6.92 us (4%)
  starting transfers between devices  6.58 us (4%)
    psum x1, blocking collectives, per_device(): stacked = lax.psum(jnp.stack(totals), ('face', 'sub'))  39.2 us
    all_gather x2, blocking collectives, fold_rows(): lax.all_gather(weight, 'sub', axis=0, tiled=True)  24 us
    all_gather x1, blocking collectives, per_device(): lax.all_gather(grid_weight, 'sub', axis=1, tiled=True)  12.5 us
    dot_general x2, matrix products, fold_rows(): jnp.dot(operand, lax.all_gather(weight, 'sub', axis=0, tiled=True), prefe...  10.5 us
    gather x1, local copies, waits for them, and re-layouts, per_device(): jnp.take(node_table, senders, axis=0)  7.54 us
    gather x1, local copies, waits for them, and re-layouts, per_device(): receiving_rows = jnp.take(latent, receivers, axis=0)  7.53 us
    ppermute x4, starting transfers between devices, passed_along(): return lax.ppermute(value, axis, pairs)  6.47 us
    all_gather x2, waiting for transfers between devices, fold_rows(): lax.all_gather(weight, 'sub', axis=0, tiled=True)  4.85 us
  transfers between devices with their start and end apart: 7, of which 1 were waited for; matrix products, arithmetic and copies ran while one was open for 31% of the time, Pallas kernels for 0%

commit v1 on v0

v1 whole, which is shorter than its diff:
```python
import functools

import jax
import jax.numpy as jnp
from jax import lax
from jax.experimental import pallas as pl
from jax.experimental.pallas import tpu as pltpu
from jax.sharding import PartitionSpec as P

MESH = pl.DeviceIdType.MESH
CHUNK = 256
BF = jnp.bfloat16
F32 = jnp.float32


def silu(v):
    return v / (1.0 + jnp.exp(-v))


def mm(a, b):
    return jnp.dot(a, b, preferred_element_type=F32)


def mm_t(a, b):
    return lax.dot_general(a, b, (((0,), (0,)), ((), ())), preferred_element_type=F32)


def hot(rows, index):
    ids = lax.broadcasted_iota(jnp.int32, (rows, index.shape[1]), 0)
    return jnp.where(ids == index, 1.0, 0.0).astype(BF)


def kernel(
    n_face, n_sub,
    mesh_ref, edge_hbm, grid_ref, send_ref, recv_ref, lists_ref, src_ref, dst_ref, area_ref,
    wg, we, w1, w2, v1, v2,
    lat_out, edge_hbm_out, mass_out,
    gg, ge, g1, g2, h1, h2,
    edges, picks, back, table, proj, halo, sums_a, sums_b, total,
    s1, r1, s2, r2, hs, hr, as_, ar, bs, br, ein, eout,
):
    face, sub = lax.axis_index("face"), lax.axis_index("sub")
    core = lax.rem(face, 2)
    partner = face + 1 - 2 * core
    nodes, width = mesh_ref.shape
    chunks = edges.shape[0] // CHUNK

    def load_edges(i):
        rows = pl.ds(pl.multiple_of(i * CHUNK, CHUNK), CHUNK)
        return pltpu.make_async_copy(edge_hbm.at[rows], edges.at[rows], ein.at[i])

    def store_edges(i):
        rows = pl.ds(pl.multiple_of(i * CHUNK, CHUNK), CHUNK)
        return pltpu.make_async_copy(edges.at[rows], edge_hbm_out.at[rows], eout.at[i])

    for i in range(chunks):
        load_edges(i).start()

    barrier = pltpu.get_barrier_semaphore()
    for k in range(1, n_sub):
        pl.semaphore_signal(barrier, inc=1, device_id=(face, lax.rem(sub + k, n_sub)), device_id_type=MESH)
    for k in range(1, n_face):
        pl.semaphore_signal(barrier, inc=1, device_id=(lax.rem(face + k, n_face), sub), device_id_type=MESH)
    pl.semaphore_wait(barrier, n_sub + n_face - 2)

    shards = [wg, we, w1.at[0], w2.at[0], v1.at[0], v2.at[0]]
    wholes = [gg, ge, g1, g2, h1, h2]

    def half_of(w, owner):
        rows = shards[w].shape[0]
        half = rows // 2
        if w == 0:
            return gg.at[owner, pl.ds(pl.multiple_of(core * half, half), half)]
        return wholes[w].at[pl.ds(pl.multiple_of(owner * rows + core * half, half), half)]

    def outward(w, k):
        half = shards[w].shape[0] // 2
        return pltpu.make_async_remote_copy(
            src_ref=shards[w].at[pl.ds(pl.multiple_of(core * half, half), half)],
            dst_ref=half_of(w, sub),
            send_sem=s1.at[w, k], recv_sem=r1.at[w, k],
            device_id=(face, lax.rem(sub + k, n_sub)), device_id_type=MESH)

    def across(w, k):
        part = half_of(w, lax.rem(sub + n_sub - k, n_sub))
        return pltpu.make_async_remote_copy(
            src_ref=part, dst_ref=part, send_sem=s2.at[w, k], recv_sem=r2.at[w, k],
            device_id=(partner, sub), device_id_type=MESH)

    for w in range(6):
        for k in range(1, n_sub):
            outward(w, k).start()

    def pass_on(w):
        for k in range(1, n_sub):
            outward(w, k).wait_recv()
            across(w, k).start()

    def arrive(w):
        for k in range(1, n_sub):
            across(w, k).wait_recv()

    gg[sub] = wg[...]
    for w in range(1, 6):
        rows = shards[w].shape[0]
        wholes[w][pl.ds(pl.multiple_of(sub * rows, rows), rows), :] = shards[w][...]
    slots = nodes + 4 * halo.shape[1]

    def mark(i, carry):
        cols = pl.ds(pl.multiple_of(i * CHUNK, CHUNK), CHUNK)
        here = hot(nodes, recv_ref[:, cols])
        back[:, cols] = here
        both = jnp.concatenate([hot(slots, send_ref[:, cols]), here], axis=0)
        picks[cols, :] = both.T
        return carry

    lax.fori_loop(0, chunks, mark, 0)
    to_node = hot(nodes, dst_ref[...])
    link_pick = jnp.concatenate([hot(grid_ref.shape[0], src_ref[...]), to_node], axis=0)

    pass_on(0)
    arrive(0)
    grid = jnp.concatenate([mm(grid_ref[...], gg[j]) for j in range(n_sub)], axis=1)
    grid = silu(grid).astype(BF)
    pass_on(1)
    arrive(1)
    rows = grid_ref.shape[0]
    from_grid = mm(grid, ge[:width, :]).astype(BF)
    from_mesh = mm(mesh_ref[...], ge[width:, :]).astype(BF)
    message = silu(mm_t(link_pick, jnp.concatenate([from_grid, from_mesh], axis=0))).astype(BF)
    latent = (mesh_ref[...].astype(F32) + mm(to_node, message)).astype(BF)
    table[...] = latent

    size = halo.shape[1]
    for d in range(4):
        halo[d] = mm_t(hot(nodes, lists_ref[0, d:d + 1, :]), latent).astype(BF)

    def border(d):
        step = (1, n_face - 1, 1, n_sub - 1)[d]
        to = (lax.rem(face + step, n_face), sub) if d < 2 else (face, lax.rem(sub + step, n_sub))
        return pltpu.make_async_remote_copy(
            src_ref=halo.at[d], dst_ref=halo.at[4 + d], send_sem=hs.at[d], recv_sem=hr.at[d],
            device_id=to, device_id_type=MESH)

    for d in range(4):
        border(d).start()

    pass_on(2)
    arrive(2)
    proj[:nodes, :] = mm(latent, g1[width:2 * width, :]).astype(BF)
    proj[slots:, :] = mm(latent, g1[2 * width:, :]).astype(BF)
    for d in range(4):
        border(d).wait_recv()
    outer = jnp.concatenate([halo[4 + d] for d in range(4)], axis=0)
    proj[nodes:slots, :] = mm(outer, g1[width:2 * width, :]).astype(BF)
    pass_on(3)
    arrive(3)

    total[...] = jnp.zeros_like(total)
    for i in range(chunks):
        load_edges(i).wait()

    def update(i, carry):
        cols = pl.ds(pl.multiple_of(i * CHUNK, CHUNK), CHUNK)
        edge = edges[cols, :]
        before = mm(edge, g1[:width, :]) + mm(picks[cols, :], proj[...])
        hidden = silu(before).astype(BF)
        new = (edge.astype(F32) + mm(hidden, g2[...])).astype(BF)
        edges[cols, :] = new
        total[...] += mm(back[:, cols], new)
        return carry

    lax.fori_loop(0, chunks // 2, update, 0)
    pass_on(4)
    lax.fori_loop(chunks // 2, chunks, update, 0)
    pass_on(5)
    for i in range(chunks):
        store_edges(i).start()
    arrive(4)
    incoming = total[...].astype(BF)
    hidden = silu(mm(table[...], h1[:width, :]) + mm(incoming, h1[width:, :])).astype(BF)
    arrive(5)
    final = (table[...].astype(F32) + mm(hidden, h2[...])).astype(BF)
    lat_out[...] = final
    part = jnp.dot(area_ref[...], final.astype(F32), precision=lax.Precision.HIGHEST, preferred_element_type=F32)

    def share_sub(k):
        return pltpu.make_async_remote_copy(
            src_ref=sums_a.at[sub], dst_ref=sums_a.at[sub], send_sem=as_.at[k], recv_sem=ar.at[k],
            device_id=(face, lax.rem(sub + k, n_sub)), device_id_type=MESH)

    def share_face(k):
        return pltpu.make_async_remote_copy(
            src_ref=sums_b.at[face], dst_ref=sums_b.at[face], send_sem=bs.at[k], recv_sem=br.at[k],
            device_id=(lax.rem(face + k, n_face), sub), device_id_type=MESH)

    sums_a[sub] = part
    for k in range(1, n_sub):
        share_sub(k).start()
    for k in range(1, n_sub):
        share_sub(k).wait_recv()
    sums_b[face] = jnp.sum(sums_a[...], axis=0)
    for k in range(1, n_face):
        share_face(k).start()
    for k in range(1, n_face):
        share_face(k).wait_recv()
    mass_out[...] = jnp.sum(sums_b[...], axis=0) / (nodes * n_face * n_sub)

    for w in range(6):
        for k in range(1, n_sub):
            outward(w, k).wait_send()
            across(w, k).wait_send()
    for d in range(4):
        border(d).wait_send()
    for k in range(1, n_sub):
        share_sub(k).wait_send()
    for k in range(1, n_face):
        share_face(k).wait_send()
    for i in range(chunks):
        store_edges(i).wait()


def per_device(
    mesh_latent, edge_latent, grid_features, senders, receivers, send_lists, link_sources,
    link_targets, node_area, grid_weight, encode_weight, edge_first, edge_second, node_first,
    node_second,
):
    n_face, n_sub = lax.axis_size("face"), lax.axis_size("sub")
    nodes, width = mesh_latent.shape
    count = edge_latent.shape[0]
    size = send_lists.shape[2]
    slots = nodes + 4 * size
    chunks = count // CHUNK
    dma = pltpu.SemaphoreType.DMA
    vmem = pl.BlockSpec(memory_space=pltpu.VMEM)
    hbm = pl.BlockSpec(memory_space=pl.ANY)
    whole = [pltpu.VMEM((n_sub * w.shape[-2], width), BF)
             for w in (encode_weight, edge_first, edge_second, node_first, node_second)]
    return pl.pallas_call(
        functools.partial(kernel, n_face, n_sub),
        out_shape=(
            jax.ShapeDtypeStruct(mesh_latent.shape, BF),
            jax.ShapeDtypeStruct(edge_latent.shape, BF),
            jax.ShapeDtypeStruct((1, width), F32),
        ),
        in_specs=[vmem, hbm] + [vmem] * 13,
        out_specs=(vmem, hbm, vmem),
        scratch_shapes=[
            pltpu.VMEM((n_sub,) + grid_weight.shape, BF), *whole,
            pltpu.VMEM(edge_latent.shape, BF),
            pltpu.VMEM((count, slots + nodes), BF),
            pltpu.VMEM((nodes, count), BF),
            pltpu.VMEM((nodes, width), BF),
            pltpu.VMEM((slots + nodes, width), BF),
            pltpu.VMEM((8, size, width), BF),
            pltpu.VMEM((n_sub, 1, width), F32),
            pltpu.VMEM((n_face, 1, width), F32),
            pltpu.VMEM((nodes, width), F32),
            dma((6, n_sub)), dma((6, n_sub)), dma((6, n_sub)), dma((6, n_sub)),
            dma((4,)), dma((4,)), dma((n_sub,)), dma((n_sub,)), dma((n_face,)), dma((n_face,)),
            dma((chunks,)), dma((chunks,)),
        ],
        compiler_params=pltpu.CompilerParams(
            collective_id=0, has_side_effects=True, vmem_limit_bytes=48 * 1024 * 1024
        ),
    )(
        mesh_latent, edge_latent, grid_features, senders.reshape(1, -1), receivers.reshape(1, -1),
        send_lists, link_sources.reshape(1, -1), link_targets.reshape(1, -1),
        node_area.reshape(1, -1), grid_weight, encode_weight, edge_first, edge_second, node_first,
        node_second,
    )


def solution(mesh):
    both = P(("face", "sub"))
    in_specs = (both,) * 9 + (P(None, "sub"), P("sub", None)) + (P(None, "sub", None),) * 4
    return jax.shard_map(
        per_device, mesh=mesh, in_specs=in_specs, out_specs=(both, both, P()), check_vma=False
    )
```

time: 155 us -> 70.8 us (0.46)
  blocking collectives: 75.8 us -> 0 us
  Pallas kernels: 0 us -> 55.4 us
  matrix products: 15.3 us -> 0 us
  between operations: 14 us -> 0.67 us
  other arithmetic: 12.7 us -> 0 us
  local copies, waits for them, and re-layouts: 22.6 us -> 14.2 us
  waiting for transfers between devices: 6.92 us -> 0 us
  starting transfers between devices: 6.58 us -> 0 us
    pallas_call x0 -> x1, Pallas kernels: none -> 55.4 us  [per_device(): pl.pallas_call(functools.partial(kernel, n_face, n_sub), out_shape=(jax.S...]
    psum x1 -> x0, blocking collectives: 39.2 us -> none  [per_device(): stacked = lax.psum(jnp.stack(totals), ('face', 'sub'))]
    all_gather x3 -> x0, blocking collectives: 36.6 us -> none  [the longest x2 24 us: fold_rows(): lax.all_gather(weight, 'sub', axis=0, tiled=True)]
    gather x5 -> x0, local copies, waits for them, and re-layouts: 19.9 us -> none  [the longest x1 7.54 us: per_device(): jnp.take(node_table, senders, axis=0)]
    dot_general x6 -> x0, matrix products: 15.3 us -> none  [the longest x2 10.5 us: fold_rows(): jnp.dot(operand, lax.all_gather(weight, 'sub', axis=0, tiled=True), prefe...]
    unnamed x21 -> x31, local copies, waits for them, and re-layouts: 2 us -> 14.2 us
    ppermute x4 -> x0, starting transfers between devices: 6.47 us -> none  [passed_along(): return lax.ppermute(value, axis, pairs)]
    select_n x6 -> x0, other arithmetic: 5.45 us -> none  [the longest x1 2.21 us: per_device(): receiving_rows = jnp.take(latent, receivers, axis=0)]
  transfers between devices with their start and end apart: 7 -> 0, of which waited for: 1 -> 0; matrix products, arithmetic and copies ran while one was open for 31% -> 0% of each run, Pallas kernels for 0% -> 0%
where the time goes in v1:
time: 70.8 us; the launch traced here: 70.3 us
  Pallas kernels  55.4 us (78%)
  local copies, waits for them, and re-layouts  14.2 us (20%)
    pallas_call x1, Pallas kernels, per_device(): pl.pallas_call(functools.partial(kernel, n_face, n_sub), out_shape=(jax.S...  55.4 us
    unnamed x31, local copies, waits for them, and re-layouts  14.2 us

profile of v1, /device:TPU:0, one launch (start us, length us, event | category | flops | bytes accessed | tf_op | source)
XLA Modules:
  0.0 70.3 jit_solution(15298174198965168577)
XLA Ops:
  0.6 0.0 copy-start
  0.6 1.0 %copy-done = bf16[1,384,512]{2,1,0:T(8,128)(2,1)S(1)} copy-done((bf16[1,384,512]{2,1,0:T(8,128)(2,1)S(1)}, bf16[1,384,512]{2,1,0:T(8,128)(2,1)}, u32[]{:S(2)}) %copy-start) | copy-done | bytes 393240
  1.6 0.0 copy-start.1
  1.6 0.9 %copy-done.1 = bf16[256,512]{1,0:T(8,128)(2,1)S(1)} copy-done((bf16[256,512]{1,0:T(8,128)(2,1)S(1)}, bf16[256,512]{1,0:T(8,128)(2,1)}, u32[]{:S(2)}) %copy-start.1) | copy-done | bytes 262168
  2.6 0.0 copy-start.2
  2.6 0.9 %copy-done.2 = bf16[256,512]{1,0:T(8,128)(2,1)S(1)} copy-done((bf16[256,512]{1,0:T(8,128)(2,1)S(1)}, bf16[256,512]{1,0:T(8,128)(2,1)}, u32[]{:S(2)}) %copy-start.2) | copy-done | bytes 262168
  3.5 0.0 copy-start.3
  3.5 0.9 %copy-done.3 = bf16[1,256,512]{2,1,0:T(8,128)(2,1)S(1)} copy-done((bf16[1,256,512]{2,1,0:T(8,128)(2,1)S(1)}, bf16[1,256,512]{2,1,0:T(8,128)(2,1)}, u32[]{:S(2)}) %copy-start.3) | copy-done | bytes 262168
  4.5 0.0 copy-start.4
  4.5 0.9 %copy-done.4 = bf16[256,384]{1,0:T(8,128)(2,1)S(1)} copy-done((bf16[256,384]{1,0:T(8,128)(2,1)S(1)}, bf16[256,384]{1,0:T(8,128)(2,1)}, u32[]{:S(2)}) %copy-start.4) | copy-done | bytes 196632
  5.4 0.0 copy-start.5
  5.4 0.9 %copy-done.5 = bf16[1,128,512]{2,1,0:T(8,128)(2,1)S(1)} copy-done((bf16[1,128,512]{2,1,0:T(8,128)(2,1)S(1)}, bf16[1,128,512]{2,1,0:T(8,128)(2,1)}, u32[]{:S(2)}) %copy-start.5) | copy-done | bytes 131096
  6.3 0.0 copy-start.6
  6.3 0.9 %copy-done.6 = bf16[1,128,512]{2,1,0:T(8,128)(2,1)S(1)} copy-done((bf16[1,128,512]{2,1,0:T(8,128)(2,1)S(1)}, bf16[1,128,512]{2,1,0:T(8,128)(2,1)}, u32[]{:S(2)}) %copy-start.6) | copy-done | bytes 131096
  7.2 0.0 copy-start.7
  7.2 0.9 %copy-done.7 = bf16[384,128]{1,0:T(8,128)(2,1)S(1)} copy-done((bf16[384,128]{1,0:T(8,128)(2,1)S(1)}, bf16[384,128]{1,0:T(8,128)(2,1)}, u32[]{:S(2)}) %copy-start.7) | copy-done | bytes 98328
  8.1 0.0 copy-start.8
  8.1 0.7 copy-done.8
  8.8 0.0 copy-start.9
  8.8 0.7 copy-done.9
  9.5 0.0 copy-start.10
  9.5 0.7 copy-done.10
  10.2 0.0 copy-start.11
  10.2 0.7 copy-done.11
  10.9 0.0 copy-start.12
  10.9 0.7 copy-done.12
  11.6 0.0 copy-start.13
  11.6 0.7 copy-done.13
  12.2 55.4 %shard_map.166 = (bf16[256,512]{1,0:T(8,128)(2,1)S(1)}, bf16[2048,512]{1,0:T(8,128)(2,1)S(1)}, f32[1,512]{1,0:T(1,128)S(1)}) custom-call(bf16[256,512]{1,0:T(8,128)(2,1)S(1)} %copy-done.1, bf16[2048,512]{1,0:T(8,128)(2,1)} %edge_hbm.1, bf16[256,384]{1,0:T(8,128)(2,1)S(1)} %copy-done.4, s32[1,2048]{1,0:T(1,128)S(1)} %bitcast.5, s32[1,2048]{1,0:T(1,128)S(1)} %bitcast.6, ...), custom_call_target="tpu_custom_call" | custom-call | tf_op jit(solution)/shard_map/pallas_call | solution.py:239
  67.7 0.7 %copy.21 = bf16[256,512]{1,0:T(8,128)(2,1)} copy(bf16[256,512]{1,0:T(8,128)(2,1)S(1)} %get-tuple-element.6) | data formatting | bytes 524288
  68.4 1.3 %copy.22 = bf16[2048,512]{1,0:T(8,128)(2,1)} copy(bf16[2048,512]{1,0:T(8,128)(2,1)S(1)} %get-tuple-element.7) | data formatting | bytes 4194304
  69.7 0.6 copy.23
Async XLA Ops:
  0.6 1.0 %copy-start = (bf16[1,384,512]{2,1,0:T(8,128)(2,1)S(1)}, bf16[1,384,512]{2,1,0:T(8,128)(2,1)}, u32[]{:S(2)}) copy-start(bf16[1,384,512]{2,1,0:T(8,128)(2,1)} %w1.1) | copy-start | bytes 1179652
  1.6 0.9 %copy-start.1 = (bf16[256,512]{1,0:T(8,128)(2,1)S(1)}, bf16[256,512]{1,0:T(8,128)(2,1)}, u32[]{:S(2)}) copy-start(bf16[256,512]{1,0:T(8,128)(2,1)} %mesh_ref.1) | copy-start | bytes 786436
  2.6 0.9 %copy-start.2 = (bf16[256,512]{1,0:T(8,128)(2,1)S(1)}, bf16[256,512]{1,0:T(8,128)(2,1)}, u32[]{:S(2)}) copy-start(bf16[256,512]{1,0:T(8,128)(2,1)} %we.1) | copy-start | bytes 786436
  3.5 0.9 %copy-start.3 = (bf16[1,256,512]{2,1,0:T(8,128)(2,1)S(1)}, bf16[1,256,512]{2,1,0:T(8,128)(2,1)}, u32[]{:S(2)}) copy-start(bf16[1,256,512]{2,1,0:T(8,128)(2,1)} %v1.1) | copy-start | bytes 786436
  4.5 0.9 %copy-start.4 = (bf16[256,384]{1,0:T(8,128)(2,1)S(1)}, bf16[256,384]{1,0:T(8,128)(2,1)}, u32[]{:S(2)}) copy-start(bf16[256,384]{1,0:T(8,128)(2,1)} %grid_ref.1) | copy-start | bytes 589828
  5.4 0.9 %copy-start.5 = (bf16[1,128,512]{2,1,0:T(8,128)(2,1)S(1)}, bf16[1,128,512]{2,1,0:T(8,128)(2,1)}, u32[]{:S(2)}) copy-start(bf16[1,128,512]{2,1,0:T(8,128)(2,1)} %w2.1) | copy-start | bytes 393220
  6.3 0.9 %copy-start.6 = (bf16[1,128,512]{2,1,0:T(8,128)(2,1)S(1)}, bf16[1,128,512]{2,1,0:T(8,128)(2,1)}, u32[]{:S(2)}) copy-start(bf16[1,128,512]{2,1,0:T(8,128)(2,1)} %v2.1) | copy-start | bytes 393220
  7.2 0.9 %copy-start.7 = (bf16[384,128]{1,0:T(8,128)(2,1)S(1)}, bf16[384,128]{1,0:T(8,128)(2,1)}, u32[]{:S(2)}) copy-start(bf16[384,128]{1,0:T(8,128)(2,1)} %wg.1) | copy-start | bytes 294916
  8.1 0.7 copy-start.8
  8.8 0.7 copy-start.9
  9.5 0.7 copy-start.10
  10.2 0.7 copy-start.11
  10.9 0.7 copy-start.12
  11.6 0.7 copy-start.13

commit v2 on v1

--- a/solution.py
+++ b/solution.py
@@ -8,7 +8,8 @@
 from jax.sharding import PartitionSpec as P
 
 MESH = pl.DeviceIdType.MESH
-CHUNK = 256
+CHUNK = 512
+QUARTERED = (1, 2, 4)
 BF = jnp.bfloat16
 F32 = jnp.float32
 
@@ -32,16 +33,19 @@
 
 def kernel(
     n_face, n_sub,
-    mesh_ref, edge_hbm, grid_ref, send_ref, recv_ref, lists_ref, src_ref, dst_ref, area_ref,
+    mesh_hbm, edge_hbm, grid_hbm, send_hbm, recv_hbm, lists_hbm, src_hbm, dst_hbm, area_hbm,
     wg, we, w1, w2, v1, v2,
     lat_out, edge_hbm_out, mass_out,
     gg, ge, g1, g2, h1, h2,
+    mesh_ref, grid_ref, send_ref, recv_ref, lists_ref, src_ref, dst_ref, area_ref,
     edges, picks, back, table, proj, halo, sums_a, sums_b, total,
-    s1, r1, s2, r2, hs, hr, as_, ar, bs, br, ein, eout,
+    s1, r1, s2, r2, s3, r3, hs, hr, as_, ar, bs, br, ein, eout, win, pin,
 ):
     face, sub = lax.axis_index("face"), lax.axis_index("sub")
     core = lax.rem(face, 2)
     partner = face + 1 - 2 * core
+    level = lax.rem(face // 2, 2)
+    beside = face + 2 - 4 * level
     nodes, width = mesh_ref.shape
     chunks = edges.shape[0] // CHUNK
 
@@ -53,6 +57,21 @@
         rows = pl.ds(pl.multiple_of(i * CHUNK, CHUNK), CHUNK)
         return pltpu.make_async_copy(edges.at[rows], edge_hbm_out.at[rows], eout.at[i])
 
+    shards = [wg, we, w1.at[0], w2.at[0], v1.at[0], v2.at[0]]
+    wholes = [gg, ge, g1, g2, h1, h2]
+
+    def own(w):
+        rows = shards[w].shape[0]
+        slot = gg.at[sub] if w == 0 else wholes[w].at[pl.ds(pl.multiple_of(sub * rows, rows), rows)]
+        return pltpu.make_async_copy(shards[w], slot, win.at[w])
+
+    pairs = [(send_hbm, send_ref), (recv_hbm, recv_ref), (src_hbm, src_ref), (dst_hbm, dst_ref),
+             (grid_hbm, grid_ref), (mesh_hbm, mesh_ref), (lists_hbm, lists_ref), (area_hbm, area_ref)]
+    loads = [pltpu.make_async_copy(a, b, pin.at[i]) for i, (a, b) in enumerate(pairs)]
+    for w in range(6):
+        own(w).start()
+    for copy in loads:
+        copy.start()
     for i in range(chunks):
         load_edges(i).start()
 
@@ -63,9 +82,6 @@
         pl.semaphore_signal(barrier, inc=1, device_id=(lax.rem(face + k, n_face), sub), device_id_type=MESH)
     pl.semaphore_wait(barrier, n_sub + n_face - 2)
 
-    shards = [wg, we, w1.at[0], w2.at[0], v1.at[0], v2.at[0]]
-    wholes = [gg, ge, g1, g2, h1, h2]
-
     def half_of(w, owner):
         rows = shards[w].shape[0]
         half = rows // 2
@@ -73,37 +89,61 @@
             return gg.at[owner, pl.ds(pl.multiple_of(core * half, half), half)]
         return wholes[w].at[pl.ds(pl.multiple_of(owner * rows + core * half, half), half)]
 
+    def quarter_of(w, owner):
+        rows = shards[w].shape[0]
+        piece = rows // 4
+        start = (core * 2 + level) * piece
+        if w == 0:
+            return gg.at[owner, pl.ds(pl.multiple_of(start, piece), piece)]
+        return wholes[w].at[pl.ds(pl.multiple_of(owner * rows + start, piece), piece)]
+
     def outward(w, k):
-        half = shards[w].shape[0] // 2
-        return pltpu.make_async_remote_copy(
-            src_ref=shards[w].at[pl.ds(pl.multiple_of(core * half, half), half)],
-            dst_ref=half_of(w, sub),
+        part = quarter_of(w, sub) if w in QUARTERED else half_of(w, sub)
+        return pltpu.make_async_remote_copy(
+            src_ref=part, dst_ref=part,
             send_sem=s1.at[w, k], recv_sem=r1.at[w, k],
             device_id=(face, lax.rem(sub + k, n_sub)), device_id_type=MESH)
 
+    def upward(w, k):
+        part = quarter_of(w, lax.rem(sub + n_sub - k, n_sub))
+        return pltpu.make_async_remote_copy(
+            src_ref=part, dst_ref=part, send_sem=s3.at[w, k], recv_sem=r3.at[w, k],
+            device_id=(beside, sub), device_id_type=MESH)
+
     def across(w, k):
         part = half_of(w, lax.rem(sub + n_sub - k, n_sub))
         return pltpu.make_async_remote_copy(
             src_ref=part, dst_ref=part, send_sem=s2.at[w, k], recv_sem=r2.at[w, k],
             device_id=(partner, sub), device_id_type=MESH)
 
-    for w in range(6):
+    def send(w):
+        own(w).wait()
         for k in range(1, n_sub):
             outward(w, k).start()
 
+    for w in range(4):
+        send(w)
+    for copy in loads:
+        copy.wait()
+
+    def climb(w):
+        for k in range(1, n_sub):
+            if w in QUARTERED:
+                outward(w, k).wait_recv()
+                upward(w, k).start()
+
     def pass_on(w):
         for k in range(1, n_sub):
-            outward(w, k).wait_recv()
+            if w in QUARTERED:
+                upward(w, k).wait_recv()
+            else:
+                outward(w, k).wait_recv()
             across(w, k).start()
 
     def arrive(w):
         for k in range(1, n_sub):
             across(w, k).wait_recv()
 
-    gg[sub] = wg[...]
-    for w in range(1, 6):
-        rows = shards[w].shape[0]
-        wholes[w][pl.ds(pl.multiple_of(sub * rows, rows), rows), :] = shards[w][...]
     slots = nodes + 4 * halo.shape[1]
 
     def mark(i, carry):
@@ -119,10 +159,12 @@
     link_pick = jnp.concatenate([hot(grid_ref.shape[0], src_ref[...]), to_node], axis=0)
 
     pass_on(0)
+    climb(1)
     arrive(0)
     grid = jnp.concatenate([mm(grid_ref[...], gg[j]) for j in range(n_sub)], axis=1)
     grid = silu(grid).astype(BF)
     pass_on(1)
+    climb(2)
     arrive(1)
     rows = grid_ref.shape[0]
     from_grid = mm(grid, ge[:width, :]).astype(BF)
@@ -144,6 +186,8 @@
 
     for d in range(4):
         border(d).start()
+    send(4)
+    send(5)
 
     pass_on(2)
     arrive(2)
@@ -171,8 +215,9 @@
         return carry
 
     lax.fori_loop(0, chunks // 2, update, 0)
+    climb(4)
+    lax.fori_loop(chunks // 2, chunks, update, 0)
     pass_on(4)
-    lax.fori_loop(chunks // 2, chunks, update, 0)
     pass_on(5)
     for i in range(chunks):
         store_edges(i).start()
@@ -210,6 +255,8 @@
         for k in range(1, n_sub):
             outward(w, k).wait_send()
             across(w, k).wait_send()
+            if w in QUARTERED:
+                upward(w, k).wait_send()
     for d in range(4):
         border(d).wait_send()
     for k in range(1, n_sub):
@@ -243,10 +290,16 @@
             jax.ShapeDtypeStruct(edge_latent.shape, BF),
             jax.ShapeDtypeStruct((1, width), F32),
         ),
-        in_specs=[vmem, hbm] + [vmem] * 13,
+        in_specs=[hbm] * 15,
         out_specs=(vmem, hbm, vmem),
         scratch_shapes=[
             pltpu.VMEM((n_sub,) + grid_weight.shape, BF), *whole,
+            pltpu.VMEM(mesh_latent.shape, BF), pltpu.VMEM(grid_features.shape, BF),
+            pltpu.VMEM((1, count), jnp.int32), pltpu.VMEM((1, count), jnp.int32),
+            pltpu.VMEM(send_lists.shape, jnp.int32),
+            pltpu.VMEM((1, link_sources.shape[0]), jnp.int32),
+            pltpu.VMEM((1, link_targets.shape[0]), jnp.int32),
+            pltpu.VMEM((1, nodes), F32),
             pltpu.VMEM(edge_latent.shape, BF),
             pltpu.VMEM((count, slots + nodes), BF),
             pltpu.VMEM((nodes, count), BF),
@@ -256,12 +309,12 @@
             pltpu.VMEM((n_sub, 1, width), F32),
             pltpu.VMEM((n_face, 1, width), F32),
             pltpu.VMEM((nodes, width), F32),
-            dma((6, n_sub)), dma((6, n_sub)), dma((6, n_sub)), dma((6, n_sub)),
+            *[dma((6, n_sub))] * 6,
             dma((4,)), dma((4,)), dma((n_sub,)), dma((n_sub,)), dma((n_face,)), dma((n_face,)),
-            dma((chunks,)), dma((chunks,)),
+            dma((chunks,)), dma((chunks,)), dma((6,)), dma((8,)),
         ],
         compiler_params=pltpu.CompilerParams(
-            collective_id=0, has_side_effects=True, vmem_limit_bytes=48 * 1024 * 1024
+            collective_id=0, has_side_effects=True, vmem_limit_bytes=67043328
         ),
     )(
         mesh_latent, edge_latent, grid_features, senders.reshape(1, -1), receivers.reshape(1, -1),

time: 70.8 us -> 52.4 us (0.74)
  Pallas kernels: 55.4 us -> 46.2 us
  local copies, waits for them, and re-layouts: 14.2 us -> 5.3 us
    pallas_call x1, Pallas kernels: 55.4 us -> 46.2 us  [per_device(): pl.pallas_call(functools.partial(kernel, n_face, n_sub), out_shape=(jax.S...]
    unnamed x31 -> x5, local copies, waits for them, and re-layouts: 14.2 us -> 5.3 us
where the time goes in v2:
time: 52.4 us; the launch traced here: 52.2 us
  Pallas kernels  46.2 us (88%)
  local copies, waits for them, and re-layouts  5.3 us (10%)
  between operations  0.65 us (1%)
    pallas_call x1, Pallas kernels, per_device(): pl.pallas_call(functools.partial(kernel, n_face, n_sub), out_shape=(jax.S...  46.2 us
    unnamed x5, local copies, waits for them, and re-layouts  5.3 us

profile of v2, /device:TPU:0, one launch (start us, length us, event | category | flops | bytes accessed | tf_op | source)
XLA Modules:
  0.0 52.2 jit_solution(17771638315032135525)
XLA Ops:
  0.6 46.2 %shard_map.166 = (bf16[256,512]{1,0:T(8,128)(2,1)}, bf16[2048,512]{1,0:T(8,128)(2,1)}, f32[1,512]{1,0:T(1,128)}) custom-call(bf16[256,512]{1,0:T(8,128)(2,1)} %mesh_hbm.1, bf16[2048,512]{1,0:T(8,128)(2,1)} %edge_hbm.1, bf16[256,384]{1,0:T(8,128)(2,1)} %grid_hbm.1, s32[1,2048]{1,0:T(1,128)} %bitcast.5, s32[1,2048]{1,0:T(1,128)} %bitcast.6, ...), custom_call_target="tpu_custom_call" | custom-call | tf_op jit(solution)/shard_map/pallas_call | solution.py:286
  46.9 1.7 %copy.21 = bf16[256,512]{1,0:T(8,128)(2,1)} copy(bf16[256,512]{1,0:T(8,128)(2,1)} %get-tuple-element.6) | data formatting | bytes 524288
  48.6 0.0 copy-start
  48.6 3.0 %copy.22 = bf16[2048,512]{1,0:T(8,128)(2,1)} copy(bf16[2048,512]{1,0:T(8,128)(2,1)} %get-tuple-element.7) | data formatting | bytes 4194304
  51.6 0.0 copy-done
  51.6 0.6 %copy.23 = f32[1,512]{1,0:T(1,128)} copy(f32[1,512]{1,0:T(1,128)S(1)} %copy-done) | data formatting | bytes 4096
Async XLA Ops:
  48.6 3.0 %copy-start = (f32[1,512]{1,0:T(1,128)S(1)}, f32[1,512]{1,0:T(1,128)}, u32[]{:S(2)}) copy-start(f32[1,512]{1,0:T(1,128)} %get-tuple-element.8) | copy-start | bytes 6148

commit v3 on v2

--- a/solution.py
+++ b/solution.py
@@ -9,7 +9,7 @@
 
 MESH = pl.DeviceIdType.MESH
 CHUNK = 512
-QUARTERED = (1, 2, 4)
+QUARTERED = (1, 2)
 BF = jnp.bfloat16
 F32 = jnp.float32
 

time: 52.4 us -> 50.9 us (0.971)
  Pallas kernels: 46.2 us -> 44.7 us
    pallas_call x1, Pallas kernels: 46.2 us -> 44.7 us  [per_device(): pl.pallas_call(functools.partial(kernel, n_face, n_sub), out_shape=(jax.S...]
where the time goes in v3:
time: 50.9 us; the launch traced here: 50.7 us
  Pallas kernels  44.7 us (88%)
  local copies, waits for them, and re-layouts  5.3 us (10%)
  between operations  0.65 us (1%)
    pallas_call x1, Pallas kernels, per_device(): pl.pallas_call(functools.partial(kernel, n_face, n_sub), out_shape=(jax.S...  44.7 us
    unnamed x5, local copies, waits for them, and re-layouts  5.3 us

profile of v3, /device:TPU:0, one launch (start us, length us, event | category | flops | bytes accessed | tf_op | source)
XLA Modules:
  0.0 50.7 jit_solution(7028937128890408916)
XLA Ops:
  0.6 44.7 %shard_map.166 = (bf16[256,512]{1,0:T(8,128)(2,1)}, bf16[2048,512]{1,0:T(8,128)(2,1)}, f32[1,512]{1,0:T(1,128)}) custom-call(bf16[256,512]{1,0:T(8,128)(2,1)} %mesh_hbm.1, bf16[2048,512]{1,0:T(8,128)(2,1)} %edge_hbm.1, bf16[256,384]{1,0:T(8,128)(2,1)} %grid_hbm.1, s32[1,2048]{1,0:T(1,128)} %bitcast.5, s32[1,2048]{1,0:T(1,128)} %bitcast.6, ...), custom_call_target="tpu_custom_call" | custom-call | tf_op jit(solution)/shard_map/pallas_call | solution.py:286
  45.4 1.7 %copy.21 = bf16[256,512]{1,0:T(8,128)(2,1)} copy(bf16[256,512]{1,0:T(8,128)(2,1)} %get-tuple-element.6) | data formatting | bytes 524288
  47.1 0.0 copy-start
  47.1 3.0 %copy.22 = bf16[2048,512]{1,0:T(8,128)(2,1)} copy(bf16[2048,512]{1,0:T(8,128)(2,1)} %get-tuple-element.7) | data formatting | bytes 4194304
  50.1 0.0 copy-done
  50.1 0.6 %copy.23 = f32[1,512]{1,0:T(1,128)} copy(f32[1,512]{1,0:T(1,128)S(1)} %copy-done) | data formatting | bytes 4096
Async XLA Ops:
  47.1 3.0 %copy-start = (f32[1,512]{1,0:T(1,128)S(1)}, f32[1,512]{1,0:T(1,128)}, u32[]{:S(2)}) copy-start(f32[1,512]{1,0:T(1,128)} %get-tuple-element.8) | copy-start | bytes 6148
